TPU v7x, 128 devices: a whole 4x4x4 slice. The times are simulated.
128 devices in a mesh: section: 4 (over y), dp: 32 (over x, z, core).
Axes of the slice: x: 4, y: 4, z: 4, core: 2. Of those that a mesh axis runs over, the one named last changes fastest.
Arguments:
- inputs: bfloat16 [4096, 1600], P('dp'), may hold values from -6 to 6
- targets: bfloat16 [4096, 1600], P('dp'), may hold values from -6 to 6
- weight_in: bfloat16 [4, 1600, 3200], P('section'), may hold values from -0.15625 to 0.15625
- hidden_bias: float32 [4, 3200], P('section'), may hold values from -3 to 3
- norm_gain: float32 [4, 1600], P('section'), may hold values from 0.5 to 1.5
- weight_out: bfloat16 [4, 3200, 1600], P('section'), may hold values from -0.109375 to 0.109375
- current: float32 [4, 3200, 1600], P('section', 'dp')
- previous: float32 [4, 3200, 1600], P('section', 'dp')
- older_basis: float32 [2, 4, 3200, 1600], P(None, 'section', 'dp')
- beta_before: float32 [1], replicated, may hold values from 1 to 4
Outputs:
- next_vector: float32 [4, 3200, 1600], P('section', 'dp')
- tridiagonal_entries: float32 [2], replicated
All inputs are finite; a program needn't handle non-finite values.
Results may differ from a plain program's by a relative error of at most 0.012.
Values may be sent and summed in bfloat16 or wider, within the bound.
A program may use at most 192 MiB of HBM per device.

v0:
```python
from functools import partial
import functools
import jax
import jax.numpy as jnp
from jax import lax
from jax.sharding import Mesh
from jax.sharding import PartitionSpec as P

DP = ("dp_0", "dp_1", "dp_2")
SECTION_DP = ("section", "dp_0", "dp_1", "dp_2")


def laid_out(blocks, dim):
    dims = list(blocks.shape[1:])
    dims[dim] *= blocks.shape[0]
    return jnp.moveaxis(blocks, 0, dim).reshape(dims)


def gather_in_order(value, axes, turns):
    blocks = value[None]
    for k in turns:
        blocks = lax.all_gather(blocks, axes[k], axis=0, tiled=True)
    carried = [lax.axis_size(axes[k]) for k in reversed(turns)]
    blocks = blocks.reshape(*carried, *value.shape)
    turned = sorted(range(len(turns)), key=lambda place: turns[len(turns) - 1 - place])
    return blocks.transpose(*turned, *range(len(turns), blocks.ndim)).reshape(-1, *value.shape)


def gathered_by_axis(value, axes, turns, dim):
    return laid_out(gather_in_order(value, axes, turns), dim)


def from_behind(value, axis, steps):
    count = lax.axis_size(axis)
    initial, last = (max(0, -steps), min(count, count - steps))
    return lax.ppermute(value, axis, [(source, source + steps) for source in range(initial, last)])


def sent_together(arrays, axis, dim, along):
    ends, at = ([], 0)
    for a in arrays[:-1]:
        at += a.shape[along]
        ends.append(at)
    both = jnp.concatenate(arrays, axis=along)
    return tuple(jnp.split(lax.all_gather(both, axis, axis=dim, tiled=True), ends, axis=along))


def over_axes(value, axes):
    return functools.reduce(lax.psum, axes, value)


def gelu_tanh(values):
    return jax.nn.gelu(values, approximate=True)


def gelu_slope(values):
    return jax.jvp(gelu_tanh, (values,), (jnp.ones_like(values),))[1]


def gelu_bend(values):
    return jax.jvp(gelu_slope, (values,), (jnp.ones_like(values),))[1]


def normalize(values, gain_row):
    mean_value = jnp.mean(values, axis=-1, keepdims=True)
    centered = values - mean_value
    variance = jnp.mean(centered * centered, axis=-1, keepdims=True)
    return centered * lax.rsqrt(variance + 1e-05) * gain_row


def times_transposed(left, right):
    return lax.dot_general(
        left, right, (((1,), (1,)), ((), ())), preferred_element_type=jnp.float32
    )


def pick_block(stack, position):
    return lax.dynamic_index_in_dim(stack, position, 0, keepdims=False)


def store_block(stack, block, position, active):
    return jnp.where(active, lax.dynamic_update_index_in_dim(stack, block, position, 0), stack)


def body(
    inputs,
    targets,
    weight_in,
    hidden_bias,
    norm_gain,
    weight_out,
    current,
    previous,
    older_basis,
    beta_before,
):
    section_index = lax.axis_index("section")
    sections = lax.axis_size("section")
    replicas = lax.axis_size(DP)
    layer_in = weight_in[0]
    bias_row = hidden_bias[0]
    gain_row = norm_gain[0]
    layer_out = weight_out[0]
    direction = gathered_by_axis(
        current[0].astype(jnp.bfloat16), (("dp_0", "dp_1"), "dp_2"), (0, 1), 0
    )
    pieces = 2
    local_rows, width = inputs.shape
    hidden_width = layer_in.shape[1]
    block_rows = local_rows // pieces
    row_count = float(local_rows * replicas)
    blocks_in = inputs.reshape(pieces, block_rows, width)
    blocks_goal = targets.reshape(pieces, block_rows, width)
    empty_rows = jnp.zeros((block_rows, width), jnp.bfloat16)
    empty_hidden = jnp.zeros((block_rows, hidden_width), jnp.bfloat16)
    empty_pre = jnp.zeros((block_rows, hidden_width), jnp.float32)
    empty_stack = jnp.zeros((pieces, block_rows, width), jnp.bfloat16)
    hidden_stack = jnp.zeros((pieces, block_rows, hidden_width), jnp.bfloat16)
    pre_stack = jnp.zeros((pieces, block_rows, hidden_width), jnp.float32)
    kept_rows, kept_tangent = (empty_stack, empty_stack)
    final_rows, final_tangent = (empty_stack, empty_stack)
    hidden_dot_stack = hidden_stack
    preact_stack, preact_dot_stack = (pre_stack, pre_stack)
    arrived_rows, arrived_tangent = (empty_rows, empty_rows)
    tick_count = pieces + sections - 1

    def run_layer(operands):
        rows_float = operands[0].astype(jnp.float32)
        tangent_float = operands[1].astype(jnp.float32)
        normed, normed_dot = jax.jvp(
            partial(normalize, gain_row=gain_row), (rows_float,), (tangent_float,)
        )
        stacked_norm = jnp.concatenate(
            [normed.astype(jnp.bfloat16), normed_dot.astype(jnp.bfloat16)], axis=0
        )
        pre_both = jnp.dot(stacked_norm, layer_in, preferred_element_type=jnp.float32)
        preact = pre_both[:block_rows] + bias_row
        preact_dot = pre_both[block_rows:]
        hidden = gelu_tanh(preact).astype(jnp.bfloat16)
        hidden_dot = (gelu_slope(preact) * preact_dot).astype(jnp.bfloat16)
        out_both = jnp.dot(
            jnp.concatenate([hidden, hidden_dot], axis=0),
            layer_out,
            preferred_element_type=jnp.float32,
        )
        rows_out = rows_float + out_both[:block_rows]
        tangent_out = tangent_float + out_both[block_rows:]
        tangent_out = tangent_out + jnp.dot(hidden, direction, preferred_element_type=jnp.float32)
        return (
            rows_out.astype(jnp.bfloat16),
            tangent_out.astype(jnp.bfloat16),
            preact,
            preact_dot,
            hidden,
            hidden_dot,
        )

    def skip_layer(operands):
        return (empty_rows, empty_rows, empty_pre, empty_pre, empty_hidden, empty_hidden)

    for step_number in range(tick_count):
        micro_slot = step_number - section_index
        active = jnp.logical_and(micro_slot >= 0, micro_slot < pieces)
        position = jnp.clip(micro_slot, 0, pieces - 1)
        feed_rows = jnp.where(section_index == 0, pick_block(blocks_in, position), arrived_rows)
        feed_tangent = jnp.where(section_index == 0, empty_rows, arrived_tangent)
        out_rows, out_tangent, preact, preact_dot, hidden, hidden_dot = lax.cond(
            active, run_layer, skip_layer, (feed_rows, feed_tangent)
        )
        kept_rows = store_block(kept_rows, feed_rows, position, active)
        kept_tangent = store_block(kept_tangent, feed_tangent, position, active)
        final_rows = store_block(final_rows, out_rows, position, active)
        final_tangent = store_block(final_tangent, out_tangent, position, active)
        preact_stack = store_block(preact_stack, preact, position, active)
        preact_dot_stack = store_block(preact_dot_stack, preact_dot, position, active)
        hidden_stack = store_block(hidden_stack, hidden, position, active)
        hidden_dot_stack = store_block(hidden_dot_stack, hidden_dot, position, active)
        if step_number + 1 < tick_count:
            arrived_rows, arrived_tangent = from_behind((out_rows, out_tangent), "section", 1)

    def run_back(operands):
        rows_float = operands[0].astype(jnp.float32)
        tangent_float = operands[1].astype(jnp.float32)
        preact, preact_dot, grad_out, grad_dot_out = (
            operands[2],
            operands[3],
            operands[4],
            operands[5],
        )
        back_both = times_transposed(jnp.concatenate([grad_out, grad_dot_out], axis=0), layer_out)
        back_hidden = back_both[:block_rows]
        back_hidden_dot = back_both[block_rows:] + times_transposed(grad_out, direction)
        slope = gelu_slope(preact)
        pre_grad = (slope * back_hidden).astype(jnp.bfloat16)
        pre_grad_dot = (
            gelu_bend(preact) * preact_dot * back_hidden + slope * back_hidden_dot
        ).astype(jnp.bfloat16)
        norm_both = times_transposed(jnp.concatenate([pre_grad, pre_grad_dot], axis=0), layer_in)
        norm_grad = norm_both[:block_rows]
        norm_grad_dot = norm_both[block_rows:]

        def pull_back(values, cotangent):
            return jax.vjp(partial(normalize, gain_row=gain_row), values)[1](cotangent)[0]

        grad_in, grad_in_dot = jax.jvp(
            pull_back, (rows_float, norm_grad), (tangent_float, norm_grad_dot)
        )
        grad_next = (grad_out.astype(jnp.float32) + grad_in).astype(jnp.bfloat16)
        grad_dot_next = (grad_dot_out.astype(jnp.float32) + grad_in_dot).astype(jnp.bfloat16)
        return (grad_next, grad_dot_next)

    def skip_back(operands):
        return (empty_rows, empty_rows)

    grad_stack, grad_dot_stack = (empty_stack, empty_stack)
    arrived_grad, arrived_grad_dot = (empty_rows, empty_rows)
    last_section = sections - 1
    for step_number in range(tick_count):
        micro_slot = step_number - (last_section - section_index)
        active = jnp.logical_and(micro_slot >= 0, micro_slot < pieces)
        position = jnp.clip(micro_slot, 0, pieces - 1)
        top_rows = pick_block(final_rows, position).astype(jnp.float32)
        top_tangent = pick_block(final_tangent, position).astype(jnp.float32)
        goal_rows = pick_block(blocks_goal, position).astype(jnp.float32)
        own_grad = ((top_rows - goal_rows) / row_count).astype(jnp.bfloat16)
        own_grad_dot = (top_tangent / row_count).astype(jnp.bfloat16)
        feed_grad = jnp.where(section_index == last_section, own_grad, arrived_grad)
        feed_grad_dot = jnp.where(section_index == last_section, own_grad_dot, arrived_grad_dot)
        operands = (
            pick_block(kept_rows, position),
            pick_block(kept_tangent, position),
            pick_block(preact_stack, position),
            pick_block(preact_dot_stack, position),
            feed_grad,
            feed_grad_dot,
        )
        grad_next, grad_dot_next = lax.cond(active, run_back, skip_back, operands)
        grad_stack = store_block(grad_stack, feed_grad, position, active)
        grad_dot_stack = store_block(grad_dot_stack, feed_grad_dot, position, active)
        if step_number + 1 < tick_count:
            arrived_grad, arrived_grad_dot = from_behind((grad_next, grad_dot_next), "section", -1)
    hidden_rows = hidden_stack.reshape(local_rows, hidden_width)
    hidden_dot_rows = hidden_dot_stack.reshape(local_rows, hidden_width)
    grad_rows = grad_stack.reshape(local_rows, width)
    grad_dot_rows = grad_dot_stack.reshape(local_rows, width)
    hidden_share, slope_share = (
        lax.all_to_all(hidden_rows.T, DP, split_axis=0, concat_axis=1, tiled=True),
        lax.all_to_all(hidden_dot_rows.T, DP, split_axis=0, concat_axis=1, tiled=True),
    )
    gathered = sent_together((grad_rows, grad_dot_rows), DP, 0, 1)
    running = jnp.dot(slope_share, gathered[0], preferred_element_type=jnp.float32)
    hvp = (running + jnp.dot(hidden_share, gathered[1], preferred_element_type=jnp.float32))[None]
    entry_count = float(hvp.size * sections * replicas)
    basis = jnp.concatenate([older_basis, previous[None], current[None]], axis=0)
    members = basis.shape[0]
    stacked = jnp.concatenate([basis, hvp[None]], axis=0).reshape(members + 1, -1)
    local_gram = lax.dot_general(
        stacked,
        stacked,
        (((1,), (1,)), ((), ())),
        precision=lax.Precision.HIGHEST,
        preferred_element_type=jnp.float32,
    )
    gram = over_axes(local_gram, SECTION_DP) / entry_count
    basis_gram = gram[:members, :members]
    cross = gram[:members, members]
    square_hvp = gram[members, members]
    indices = jnp.arange(members)
    weights_start = jnp.where(indices == members - 2, -beta_before[0], 0.0)
    alpha_value = cross[members - 1] + jnp.sum(weights_start * basis_gram[:, members - 1])
    weights_first = weights_start - jnp.where(indices == members - 1, alpha_value, 0.0)
    coeffs = cross + jnp.sum(basis_gram * weights_first[:, None], axis=0)
    weights_second = weights_first - coeffs
    quadratic = jnp.sum(weights_second[:, None] * basis_gram * weights_second[None, :])
    square_second = square_hvp + 2.0 * jnp.sum(weights_second * cross) + quadratic
    beta_value = jnp.sqrt(jnp.maximum(square_second, 0.0) + 1e-06)
    second = hvp + jnp.sum(weights_second[:, None, None, None] * basis, axis=0)
    return (second / beta_value, jnp.stack([alpha_value, beta_value]))


def solution(mesh):
    finer = Mesh(
        mesh.devices.reshape(mesh.shape["section"], 4, 4, 2), ("section", "dp_0", "dp_1", "dp_2")
    )
    in_specs = (
        P(DP, None),
        P(DP, None),
        P("section", None, None),
        P("section", None),
        P("section", None),
        P("section", None, None),
        P("section", DP, None),
        P("section", DP, None),
        P(None, "section", DP, None),
        P(),
    )
    out_specs = (P("section", DP, None), P())
    return jax.shard_map(body, mesh=finer, in_specs=in_specs, out_specs=out_specs, check_vma=False)
```

profile of v0, /device:TPU:1, one launch (start us, length us, event | category | flops | bytes accessed | tf_op | source)
XLA Modules:
  0.0 732.1 jit_solution(5869003339484082788)
XLA Ops:
  9.1 62.4 %all-gather.4.cloned.1.call-done = bf16[16,100,1600]{2,1,0:T(8,128)(2,1)} async-done(((bf16[1,100,1600]{2,1,0:T(8,128)(2,1)}), bf16[16,100,1600]{2,1,0:T(8,128)(2,1)}) %all-gather.4.cloned.1.call-update) | async-done | bytes 5120016 | tf_op jit(solution)/shard_map/all_gather | solution.py:22
  79.4 16.9 %copy.178 = bf16[1,3200,1600]{2,1,0:T(8,128)(2,1)} copy(bf16[1,3200,1600]{1,2,0:T(8,128)(2,1)} %param.33) | data formatting | bytes 20480000 | tf_op args[5]
  103.0 10.0 %copy.280 = bf16[2,16,100,1600]{3,2,0,1:T(8,128)(2,1)} copy(bf16[2,16,100,1600]{3,1,0,2:T(8,128)(2,1)} %bitcast.647) | data formatting | bytes 20480000 | tf_op jit(solution)/shard_map/reshape | solution.py:24
  113.0 14.7 %reshape_reshape.3 = bf16[3200,1600]{1,0:T(8,128)(2,1)} reshape(bf16[16,2,100,1600]{3,2,1,0:T(8,128)(2,1)} %bitcast.644) | data formatting | bytes 20480000 | tf_op jit(solution)/shard_map/reshape;reshape | solution.py:16
  127.8 25.5 %conditional.9 = (f32[64,3200]{1,0:T(8,128)}, f32[64,3200]{1,0:T(8,128)S(1)}, bf16[1,64,3200]{2,1,0:T(8,128)(2,1)S(1)}, bf16[1,64,3200]{2,1,0:T(8,128)(2,1)}, bf...) conditional(s32[]{:T(128)} %convert_element_type.470, () %tuple.151, (bf16[1,64,1600]{2,1,0:T(8,128)(2,1)S(1)}, ...), branch_computations={%region_0.1_spmd, %region_1.5_spmd} | conditional | flops 3289190656 | bytes 78807200 | solution.py:167
  142.7 8.2 %fusion = bf16[64,1600]{0,1:T(8,128)(2,1)S(1)} fusion(bf16[64,3200]{1,0:T(8,128)(2,1)S(1)} %multiply_convert_fusion, bf16[3200,1600]{1,0:T(8,128)(2,1)} %get-tuple-element.500, f32[128,1600]{0,1:T(8,128)S(1)} %fusion.25), kind=kOutput, calls=%fused_computation.1 | convolution fusion | flops 655564800 | bytes 11264000 | tf_op jit(solution)/shard_map/cond/branch_1_fun/dot_general | solution.py:148
  164.0 34.1 %conditional.10 = (bf16[64,1600]{0,1:T(8,128)(2,1)}, bf16[64,1600]{0,1:T(8,128)(2,1)}, f32[1,64,3200]{2,1,0:T(8,128)}, f32[1,64,3200]{2,1,0:T(8,128)}, bf16[1,64...) conditional(s32[]{:T(128)} %convert_element_type.472, ...), branch_computations={%region_5.6_spmd, %region_6.11_spmd} | conditional | flops 3286835456 | bytes 77476808 | solution.py:167
  184.9 9.1 %fusion.36 = bf16[64,1600]{0,1:T(8,128)(2,1)} fusion(bf16[64,3200]{1,0:T(8,128)(2,1)} %get-tuple-element.1010, bf16[3200,1600]{1,0:T(8,128)(2,1)} %get-tuple-element.507, bf16[64,1600]{0,1:T(8,128)(2,1)S(1)} %copy-done.21, f32[128,1600]{0,1:T(8,128)S(1)} %fusion.63), kind=kOutput, calls=%fused_computation.50 | convolution fusion | flops 655769600 | bytes 11468800 | tf_op jit(solution)/shard_map/cond/branch_1_fun/dot_general | solution.py:148
  224.0 34.1 %collective-permute-start.5 = (bf16[64,1600]{1,0:T(8,128)(2,1)}, bf16[64,1600]{1,0:T(8,128)(2,1)S(1)}, u32[]{:S(2)}, u32[]{:S(2)}) collective-permute-start(bf16[64,1600]{1,0:T(8,128)(2,1)} %copy.193), channel_id=1, source_target_pairs={{0,32},{32,64},{64,96},{1,33},{33,65},{65,97},{2,34},{34,66},{66,9... | collective-permute-start | bytes 614408 | tf_op jit(solution)/shard_map/ppermute | solution.py:36
  279.8 32.4 %collective-permute-start.6 = (bf16[64,1600]{1,0:T(8,128)(2,1)}, bf16[64,1600]{1,0:T(8,128)(2,1)S(1)}, u32[]{:S(2)}, u32[]{:S(2)}) collective-permute-start(bf16[64,1600]{1,0:T(8,128)(2,1)} %copy.196), channel_id=1, source_target_pairs={{0,32},{32,64},{64,96},{1,33},{33,65},{65,97},{2,34},{34,66},{66,9... | collective-permute-start | bytes 614408 | tf_op jit(solution)/shard_map/ppermute | solution.py:36
  365.5 120.2 %collective-permute-done.13 = bf16[64,1600]{1,0:T(8,128)(2,1)S(1)} collective-permute-done((bf16[64,1600]{1,0:T(8,128)(2,1)S(1)}, bf16[64,1600]{1,0:T(8,128)(2,1)S(1)}, u32[]{:S(2)}, u32[]{:S(2)}) %collective-permute-start.13) | collective-permute-done | bytes 204832 | tf_op jit(solution)/shard_map/ppermute | solution.py:36
  493.2 27.1 %conditional.17 = (bf16[64,1600]{0,1:T(8,128)(2,1)}, bf16[64,1600]{0,1:T(8,128)(2,1)}) conditional(s32[]{:T(128)} %convert_element_type.508, () %tuple.167, (bf16[64,1600]{1,0:T(8,128)(2,1)S(1)}, f32[2,64,3200]{2,1,0:T(8,128)S(1)}, s32[]{:T(128)}, bf16[64,1600]{1,0:T(8,128)(2,1)S(1)}, bf16[3200,1600]{1,0:T(8,128)(2,1)}, ...), branch_computations={%region_59.60_spmd, %region_60.69_spmd} | conditional | flops 3295233024 | bytes 87697088 | solution.py:237
  495.6 7.7 %fusion.369 = f32[128,3200]{1,0:T(8,128)S(1)} fusion(bf16[3200,1600]{1,0:T(8,128)(2,1)} %get-tuple-element.568, bf16[64,1600]{0,1:T(8,128)(2,1)S(1)} %copy.234, bf16[64,1600]{0,1:T(8,128)(2,1)} %copy.233), kind=kOutput, calls=%fused_computation.554 | convolution fusion | flops 1311539200 | bytes 12288000 | tf_op jit(solution)/shard_map/cond/branch_1_fun/dot_general | solution.py:72
  503.4 7.4 %fusion.334 = bf16[64,3200]{1,0:T(8,128)(2,1)S(1)} fusion(bf16[64,1600]{1,0:T(8,128)(2,1)S(1)} %get-tuple-element.905, bf16[3200,1600]{1,0:T(8,128)(2,1)} %get-tuple-element.570, f32[128,3200]{1,0:T(8,128)S(1)} %fusion.369, f32[2,64,3200]{2,1,0:T(8,128)S(1)} %copy-done.6, s32[]{:T(128)} %get-tuple-element.566, f32[2,64,3200]{2,1,0:T(8,128)S(1)} %get-tuple-element.565), kind=kOutput, calls=%fused_computation.501 | convolution fusion | flops 661913600 | bytes 14131204 | tf_op jit(solution)/shard_map/cond/branch_1_fun/dot_general | solution.py:72
  542.5 9.8 %all-to-all-start = ((bf16[32,100,128]{2,1,0:T(8,128)(2,1)}), bf16[32,100,128]{2,1,0:T(8,128)(2,1)}, u32[]{:S(2)}, u32[]{:S(2)}) async-start(bf16[32,100,128]{2,1,0:T(8,128)(2,1)} %all_to_all.28), calls=%async_computation | async-start | bytes 1703936 | tf_op jit(solution)/shard_map/all_to_all | solution.py:248
  554.4 20.7 %all-to-all-done = bf16[32,100,128]{2,1,0:T(8,128)(2,1)} async-done(((bf16[32,100,128]{2,1,0:T(8,128)(2,1)}), bf16[32,100,128]{2,1,0:T(8,128)(2,1)}, u32[]{:S(2)}, u32[]{:S(2)}) %all-to-all-start) | async-done | bytes 819232 | tf_op jit(solution)/shard_map/all_to_all | solution.py:248
  585.7 12.4 %all-to-all-done.1 = bf16[32,100,128]{2,1,0:T(8,128)(2,1)S(1)} async-done(((bf16[32,100,128]{2,1,0:T(8,128)(2,1)}), bf16[32,100,128]{2,1,0:T(8,128)(2,1)S(1)}, u32[]{:S(2)}, u32[]{:S(2)}) %all-to-all-start.1) | async-done | bytes 819232 | tf_op jit(solution)/shard_map/all_to_all | solution.py:247
  598.6 51.1 %all-gather.8.cloned.1.call-done = bf16[4096,3200]{1,0:T(8,128)(2,1)} async-done(((bf16[128,3200]{1,0:T(8,128)(2,1)}), bf16[4096,3200]{1,0:T(8,128)(2,1)}) %all-gather.8.cloned.1.call-update) | async-done | bytes 26214416 | tf_op jit(solution)/shard_map/all_gather | solution.py:45
  649.8 9.1 %fusion.378 = f32[100,1600]{1,0:T(8,128)S(1)} fusion(bf16[100,4096]{1,0:T(8,128)(2,1)S(1)} %bitcast.670, bf16[4096,3200]{1,0:T(8,128)(2,1)} %all-gather.8.cloned.1.call-done), kind=kOutput, calls=%fused_computation.573 | convolution fusion | flops 1310720000 | bytes 15090688 | tf_op jit(solution)/shard_map/dot_general | solution.py:252
  658.9 7.3 fusion.390
  667.0 12.1 %fusion.393 = f32[5,5]{1,0:T(8,128)S(1)} fusion(f32[1,1,100,1600]{3,0,2,1:T(1,128)S(1)} %copy.242, f32[1,1,100,1600]{3,0,2,1:T(1,128)S(1)} %bitcast.667, f32[1,1,100,1600]{3,0,2,1:T(1,128)S(1)} %bitcast.672, f32[2,1,100,1600]{3,0,2,1:T(2,128)S(1)} %copy-done.59), kind=kOutput, calls=%fused_computation.589 | convolution fusion | flops 50400000 | bytes 3200100 | tf_op jit(solution)/shard_map/dot_general | solution.py:257
  679.0 9.0 %psum.28 = f32[5,5]{1,0:T(8,128)S(1)} all-reduce(f32[5,5]{1,0:T(8,128)S(1)} %fusion.393), channel_id=1, replica_groups=mesh['section'=4,'dp_0'=4,'dp_1'=4,'dp_2'=2] {'section'}, use_global_device_ids=true, to_apply=%region_69.70 | all-reduce | flops 25 | bytes 200 | tf_op jit(solution)/shard_map/psum | solution.py:49
  688.0 8.4 %psum.29 = f32[5,5]{1,0:T(8,128)S(1)} all-reduce(f32[5,5]{1,0:T(8,128)S(1)} %psum.28), channel_id=1, replica_groups=mesh['section'=4,'dp_0'=4,'dp_1'=4,'dp_2'=2] {'dp_0'}, use_global_device_ids=true, to_apply=%region_70.71 | all-reduce | flops 25 | bytes 200 | tf_op jit(solution)/shard_map/psum | solution.py:49
  703.0 8.4 %psum.31 = f32[5,5]{1,0:T(8,128)S(1)} all-reduce(f32[5,5]{1,0:T(8,128)S(1)} %psum.30), channel_id=1, replica_groups=mesh['section'=4,'dp_0'=4,'dp_1'=4,'dp_2'=2] {'dp_2'}, use_global_device_ids=true, to_apply=%region_72.73 | all-reduce | flops 25 | bytes 200 | tf_op jit(solution)/shard_map/psum | solution.py:49
  (328 shorter events, 258.9 us)
Async XLA Ops:
  7.2 64.4 %all-gather.4.cloned.1.call-start = ((), (), s32[]{:S(2)}) async-start(), calls=%async_computation.2 | async-start | bytes 5883904 | tf_op jit(solution)/shard_map/all_gather | solution.py:22
  9.1 93.9 %all-gather.6.cloned.1.call-start = ((), (), s32[]{:S(2)}) async-start(), calls=%async_computation.3 | async-start | bytes 15974400 | tf_op jit(solution)/shard_map/all_gather | solution.py:22
  77.2 572.6 %all-gather.8.cloned.1.call-start = ((), (), s32[]{:S(2)}) async-start(), calls=%async_computation.4 | async-start | bytes 27033600 | tf_op jit(solution)/shard_map/all_gather | solution.py:45
  78.4 18.0 %copy-start.32 = (bf16[128,1600]{1,0:T(8,128)(2,1)}, bf16[128,1600]{1,0:T(8,128)(2,1)S(1)}, u32[]{:S(2)}) copy-start(bf16[128,1600]{1,0:T(8,128)(2,1)S(1)} %copy.177) | copy-start | bytes 1228804
  153.4 6.0 collective-permute-start
  154.8 9.1 %collective-permute-start.1 = (bf16[64,1600]{1,0:T(8,128)(2,1)S(1)}, bf16[64,1600]{1,0:T(8,128)(2,1)S(1)}, u32[]{:S(2)}, u32[]{:S(2)}) collective-permute-start(bf16[64,1600]{1,0:T(8,128)(2,1)S(1)} %get-tuple-element.919), channel_id=1, source_target_pairs={{0,32},{32,64},{64,96},{1,33},{33,65},{65,97},{2,34},{34,66},{66,9... | collective-permute-start | bytes 614408 | tf_op jit(solution)/shard_map/ppermute | solution.py:36
  201.1 10.1 %collective-permute-start.3 = (bf16[64,1600]{1,0:T(8,128)(2,1)}, bf16[64,1600]{1,0:T(8,128)(2,1)S(1)}, u32[]{:S(2)}, u32[]{:S(2)}) collective-permute-start(bf16[64,1600]{1,0:T(8,128)(2,1)} %copy.189), channel_id=1, source_target_pairs={{0,32},{32,64},{64,96},{1,33},{33,65},{65,97},{2,34},{34,66},{66,9... | collective-permute-start | bytes 614408 | tf_op jit(solution)/shard_map/ppermute | solution.py:36
  205.4 8.6 %collective-permute-start.2 = (bf16[64,1600]{1,0:T(8,128)(2,1)S(1)}, bf16[64,1600]{1,0:T(8,128)(2,1)S(1)}, u32[]{:S(2)}, u32[]{:S(2)}) collective-permute-start(bf16[64,1600]{1,0:T(8,128)(2,1)S(1)} %copy.188), channel_id=1, source_target_pairs={{0,32},{32,64},{64,96},{1,33},{33,65},{65,97},{2,34},{34,66},{66,9... | collective-permute-start | bytes 614408 | tf_op jit(solution)/shard_map/ppermute | solution.py:36
  224.0 38.9 %collective-permute-start.5 = (bf16[64,1600]{1,0:T(8,128)(2,1)}, bf16[64,1600]{1,0:T(8,128)(2,1)S(1)}, u32[]{:S(2)}, u32[]{:S(2)}) collective-permute-start(bf16[64,1600]{1,0:T(8,128)(2,1)} %copy.193), channel_id=1, source_target_pairs={{0,32},{32,64},{64,96},{1,33},{33,65},{65,97},{2,34},{34,66},{66,9... | collective-permute-start | bytes 614408 | tf_op jit(solution)/shard_map/ppermute | solution.py:36
  258.1 7.8 %collective-permute-start.4 = (bf16[64,1600]{1,0:T(8,128)(2,1)}, bf16[64,1600]{1,0:T(8,128)(2,1)S(1)}, u32[]{:S(2)}, u32[]{:S(2)}) collective-permute-start(bf16[64,1600]{1,0:T(8,128)(2,1)} %copy.192), channel_id=1, source_target_pairs={{0,32},{32,64},{64,96},{1,33},{33,65},{65,97},{2,34},{34,66},{66,9... | collective-permute-start | bytes 614408 | tf_op jit(solution)/shard_map/ppermute | solution.py:36
  275.7 39.0 %collective-permute-start.7 = (bf16[64,1600]{1,0:T(8,128)(2,1)}, bf16[64,1600]{1,0:T(8,128)(2,1)S(1)}, u32[]{:S(2)}, u32[]{:S(2)}) collective-permute-start(bf16[64,1600]{1,0:T(8,128)(2,1)} %copy.197), channel_id=1, source_target_pairs={{0,32},{32,64},{64,96},{1,33},{33,65},{65,97},{2,34},{34,66},{66,9... | collective-permute-start | bytes 614408 | tf_op jit(solution)/shard_map/ppermute | solution.py:36
  279.8 35.8 %collective-permute-start.6 = (bf16[64,1600]{1,0:T(8,128)(2,1)}, bf16[64,1600]{1,0:T(8,128)(2,1)S(1)}, u32[]{:S(2)}, u32[]{:S(2)}) collective-permute-start(bf16[64,1600]{1,0:T(8,128)(2,1)} %copy.196), channel_id=1, source_target_pairs={{0,32},{32,64},{64,96},{1,33},{33,65},{65,97},{2,34},{34,66},{66,9... | collective-permute-start | bytes 614408 | tf_op jit(solution)/shard_map/ppermute | solution.py:36
  328.7 7.1 collective-permute-start.9
  330.0 9.5 %collective-permute-start.8 = (bf16[64,1600]{1,0:T(8,128)(2,1)S(1)}, bf16[64,1600]{1,0:T(8,128)(2,1)S(1)}, u32[]{:S(2)}, u32[]{:S(2)}) collective-permute-start(bf16[64,1600]{1,0:T(8,128)(2,1)S(1)} %copy.219), channel_id=1, source_target_pairs={{32,0},{64,32},{96,64},{33,1},{65,33},{97,65},{34,2},{66,34},{98,6... | collective-permute-start | bytes 614408 | tf_op jit(solution)/shard_map/ppermute | solution.py:36
  344.3 7.4 %collective-permute-start.11 = (bf16[64,1600]{1,0:T(8,128)(2,1)S(1)}, bf16[64,1600]{1,0:T(8,128)(2,1)S(1)}, u32[]{:S(2)}, u32[]{:S(2)}) collective-permute-start(bf16[64,1600]{1,0:T(8,128)(2,1)S(1)} %copy.226), channel_id=1, source_target_pairs={{32,0},{64,32},{96,64},{33,1},{65,33},{97,65},{34,2},{66,34},{98,6... | collective-permute-start | bytes 614408 | tf_op jit(solution)/shard_map/ppermute | solution.py:36
  346.8 9.9 %collective-permute-start.10 = (bf16[64,1600]{1,0:T(8,128)(2,1)S(1)}, bf16[64,1600]{1,0:T(8,128)(2,1)S(1)}, u32[]{:S(2)}, u32[]{:S(2)}) collective-permute-start(bf16[64,1600]{1,0:T(8,128)(2,1)S(1)} %copy.225), channel_id=1, source_target_pairs={{32,0},{64,32},{96,64},{33,1},{65,33},{97,65},{34,2},{66,34},{98,6... | collective-permute-start | bytes 614408 | tf_op jit(solution)/shard_map/ppermute | solution.py:36
  361.5 124.2 %collective-permute-start.13 = (bf16[64,1600]{1,0:T(8,128)(2,1)S(1)}, bf16[64,1600]{1,0:T(8,128)(2,1)S(1)}, u32[]{:S(2)}, u32[]{:S(2)}) collective-permute-start(bf16[64,1600]{1,0:T(8,128)(2,1)S(1)} %copy.232), channel_id=1, source_target_pairs={{32,0},{64,32},{96,64},{33,1},{65,33},{97,65},{34,2},{66,34},{98,6... | collective-permute-start | bytes 614408 | tf_op jit(solution)/shard_map/ppermute | solution.py:36
  364.0 127.3 %collective-permute-start.12 = (bf16[64,1600]{1,0:T(8,128)(2,1)S(1)}, bf16[64,1600]{1,0:T(8,128)(2,1)S(1)}, u32[]{:S(2)}, u32[]{:S(2)}) collective-permute-start(bf16[64,1600]{1,0:T(8,128)(2,1)S(1)} %copy.231), channel_id=1, source_target_pairs={{32,0},{64,32},{96,64},{33,1},{65,33},{97,65},{34,2},{66,34},{98,6... | collective-permute-start | bytes 614408 | tf_op jit(solution)/shard_map/ppermute | solution.py:36
  493.2 34.9 %copy-start.1 = (bf16[2,64,1600]{2,1,0:T(8,128)(2,1)S(1)}, bf16[2,64,1600]{2,1,0:T(8,128)(2,1)}, u32[]{:S(2)}) copy-start(bf16[2,64,1600]{2,1,0:T(8,128)(2,1)} %copy-done) | copy-start | bytes 1228804
  521.5 6.6 collective-permute-start.15
  524.1 9.9 %collective-permute-start.14 = (bf16[64,1600]{1,0:T(8,128)(2,1)S(1)}, bf16[64,1600]{1,0:T(8,128)(2,1)S(1)}, u32[]{:S(2)}, u32[]{:S(2)}) collective-permute-start(bf16[64,1600]{1,0:T(8,128)(2,1)S(1)} %copy.237), channel_id=1, source_target_pairs={{32,0},{64,32},{96,64},{33,1},{65,33},{97,65},{34,2},{66,34},{98,6... | collective-permute-start | bytes 614408 | tf_op jit(solution)/shard_map/ppermute | solution.py:36
  542.5 32.6 %all-to-all-start = ((bf16[32,100,128]{2,1,0:T(8,128)(2,1)}), bf16[32,100,128]{2,1,0:T(8,128)(2,1)}, u32[]{:S(2)}, u32[]{:S(2)}) async-start(bf16[32,100,128]{2,1,0:T(8,128)(2,1)} %all_to_all.28), calls=%async_computation | async-start | bytes 1703936 | tf_op jit(solution)/shard_map/all_to_all | solution.py:248
  552.5 28.8 %copy-start.30 = (f32[2,1,100,1600]{3,1,2,0:T(1,128)S(1)}, f32[2,1,100,1600]{3,1,2,0:T(1,128)}, u32[]{:S(2)}) copy-start(f32[2,1,100,1600]{3,1,2,0:T(1,128)} %param.36) | copy-start | bytes 3840004
  575.1 23.0 %all-to-all-start.1 = ((bf16[32,100,128]{2,1,0:T(8,128)(2,1)}), bf16[32,100,128]{2,1,0:T(8,128)(2,1)S(1)}, u32[]{:S(2)}, u32[]{:S(2)}) async-start(bf16[32,100,128]{2,1,0:T(8,128)(2,1)} %all_to_all.32), calls=%async_computation.1 | async-start | bytes 1703936 | tf_op jit(solution)/shard_map/all_to_all | solution.py:247
  (45 other events, 281.5 us)
Sparse Core Ops, SparseCore 0:
  10.7 60.7 all-gather.3
  77.3 25.6 all-gather.5
  538.4 111.3 all-gather.7
where the time goes:
time: 739 us; the launch traced here: 732 us
  waiting for transfers between devices  306 us (41%)
  local copies, waits for them, and re-layouts  113 us (15%)
  starting transfers between devices  108 us (15%)
  matrix products  85.4 us (12%)
  other arithmetic  66.4 us (9%)
  blocking collectives  32.3 us (4%)
  between operations  19 us (3%)
    ppermute x16, waiting for transfers between devices, from_behind(): lax.ppermute(value, axis, [(source, source + steps) for source in range(i...  153 us
    ppermute x16, starting transfers between devices, from_behind(): lax.ppermute(value, axis, [(source, source + steps) for source in range(i...  92.7 us
    all_gather x2, waiting for transfers between devices, gather_in_order(): blocks = lax.all_gather(blocks, axes[k], axis=0, tiled=True)  68.9 us
    all_gather x1, waiting for transfers between devices, sent_together(): lax.all_gather(both, axis, axis=dim, tiled=True)  51.1 us
    select_n x46, other arithmetic, store_block(): jnp.where(active, lax.dynamic_update_index_in_dim(stack, block, position,...  36.1 us
    psum x4, blocking collectives, over_axes(): return functools.reduce(lax.psum, axes, value)  32.3 us
    unnamed x76, local copies, waits for them, and re-layouts  26.7 us
    all_to_all x1, waiting for transfers between devices, body(): lax.all_to_all(hidden_dot_rows.T, DP, split_axis=0, concat_axis=1, tiled=...  20.7 us
  transfers between devices with their start and end apart: 21, of which 17 were waited for; matrix products, arithmetic and copies ran while one was open for 7% of the time, Pallas kernels for 0%

commit v1 on v0

--- a/solution.py
+++ b/solution.py
@@ -19,7 +19,9 @@
 def gather_in_order(value, axes, turns):
     blocks = value[None]
     for k in turns:
-        blocks = lax.all_gather(blocks, axes[k], axis=0, tiled=True)
+        blocks = jnp.concatenate(
+            lax.all_to_all(jnp.stack([blocks] * lax.axis_size(axes[k])), axes[k], 0, 0), axis=0
+        )
     carried = [lax.axis_size(axes[k]) for k in reversed(turns)]
     blocks = blocks.reshape(*carried, *value.shape)
     turned = sorted(range(len(turns)), key=lambda place: turns[len(turns) - 1 - place])

time: 739 us -> 769 us (1.041)
  blocking collectives: 32.3 us -> 46.7 us
  starting transfers between devices: 108 us -> 121 us
  other arithmetic: 66.4 us -> 75.8 us
    all_gather x2 -> x0, waiting for transfers between devices: 68.9 us -> none  [gather_in_order(): blocks = lax.all_gather(blocks, axes[k], axis=0, tiled=True)]
    all_to_all x0 -> x1, waiting for transfers between devices: none -> 67.7 us  [gather_in_order(): lax.all_to_all(jnp.stack([blocks] * lax.axis_size(axes[k])), axes[k], 0, 0)]
    all_to_all x0 -> x1, blocking collectives: none -> 14.3 us  [gather_in_order(): lax.all_to_all(jnp.stack([blocks] * lax.axis_size(axes[k])), axes[k], 0, 0)]
    reshape x1 -> x0, local copies, waits for them, and re-layouts: 10 us -> none  [gather_in_order(): blocks = blocks.reshape(*carried, *value.shape)]
    all_to_all x0 -> x1, starting transfers between devices: none -> 8.59 us  [gather_in_order(): lax.all_to_all(jnp.stack([blocks] * lax.axis_size(axes[k])), axes[k], 0, 0)]
    another operation x5 -> x6, other arithmetic: 0.15 us -> 8 us  [the longest x1 7.85 us: gather_in_order(): jnp.stack([blocks] * lax.axis_size(axes[k]))]
  transfers between devices with their start and end apart: 21 -> 20, of which waited for: 17 -> 16; matrix products, arithmetic and copies ran while one was open for 7% -> 7% of each run, Pallas kernels for 0% -> 0%
where the time goes in v1:
time: 769 us; the launch traced here: 761 us
  waiting for transfers between devices  304 us (40%)
  starting transfers between devices  121 us (16%)
  local copies, waits for them, and re-layouts  107 us (14%)
  matrix products  85.4 us (11%)
  other arithmetic  75.8 us (10%)
  blocking collectives  46.7 us (6%)
  between operations  19.4 us (3%)
    ppermute x16, waiting for transfers between devices, from_behind(): lax.ppermute(value, axis, [(source, source + steps) for source in range(i...  152 us
    ppermute x16, starting transfers between devices, from_behind(): lax.ppermute(value, axis, [(source, source + steps) for source in range(i...  92.8 us
    all_to_all x1, waiting for transfers between devices, gather_in_order(): lax.all_to_all(jnp.stack([blocks] * lax.axis_size(axes[k])), axes[k], 0, 0)  67.7 us
    all_gather x1, waiting for transfers between devices, sent_together(): lax.all_gather(both, axis, axis=dim, tiled=True)  51.4 us
    select_n x46, other arithmetic, store_block(): jnp.where(active, lax.dynamic_update_index_in_dim(stack, block, position,...  36 us
    psum x4, blocking collectives, over_axes(): return functools.reduce(lax.psum, axes, value)  32.3 us
    unnamed x76, local copies, waits for them, and re-layouts  23.4 us
    all_to_all x1, waiting for transfers between devices, body(): lax.all_to_all(hidden_dot_rows.T, DP, split_axis=0, concat_axis=1, tiled=...  20.7 us
  transfers between devices with their start and end apart: 20, of which 16 were waited for; matrix products, arithmetic and copies ran while one was open for 7% of the time, Pallas kernels for 0%

profile of v1, /device:TPU:1, one launch (start us, length us, event | category | flops | bytes accessed | tf_op | source)
XLA Modules:
  0.0 761.5 jit_solution(4907670609314963355)
XLA Ops:
  11.6 8.6 %all-to-all-start = ((bf16[16,1,100,1600]{3,2,1,0:T(8,128)(2,1)}), bf16[16,1,100,1600]{3,2,1,0:T(8,128)(2,1)}, u32[]{:S(2)}, u32[]{:S(2)}) async-start(bf16[16,1,100,1600]{3,2,1,0:T(8,128)(2,1)} %stack.15), calls=%async_computation | async-start | bytes 11075584 | tf_op jit(solution)/shard_map/all_to_all | solution.py:23
  21.6 16.2 %copy.102 = bf16[1,3200,1600]{2,1,0:T(8,128)(2,1)} copy(bf16[1,3200,1600]{1,2,0:T(8,128)(2,1)} %param.33) | data formatting | bytes 20480000 | tf_op args[5]
  38.0 67.7 %all-to-all-done = bf16[16,1,100,1600]{3,2,1,0:T(8,128)(2,1)} async-done(((bf16[16,1,100,1600]{3,2,1,0:T(8,128)(2,1)}), bf16[16,1,100,1600]{3,2,1,0:T(8,128)(2,1)}, u32[]{:S(2)}, u32[]{:S(2)}) %all-to-all-start) | async-done | bytes 5120032 | tf_op jit(solution)/shard_map/all_to_all | solution.py:23
  105.7 7.8 %pad_maximum_fusion = bf16[2,16,100,1600]{3,2,1,0:T(8,128)(2,1)S(1)} fusion(bf16[1,16,100,1600]{3,2,1,0:T(8,128)(2,1)} %bitcast.48), kind=kLoop, calls=%fused_computation.577 | loop fusion | flops 5120000 | bytes 15360000 | tf_op jit(solution)/shard_map/stack | solution.py:23
  117.5 14.3 %all_to_all.48 = bf16[2,16,100,1600]{3,1,2,0:T(8,128)(2,1)S(1)} all-to-all(bf16[2,16,100,1600]{3,1,2,0:T(8,128)(2,1)S(1)} %copy.103), channel_id=1, replica_groups=mesh['section'=4,'dp_0'=4,'dp_1'=4,'dp_2'=2] {'dp_2'}, dimensions={0} | all-to-all | bytes 20480000 | tf_op jit(solution)/shard_map/all_to_all | solution.py:23
  138.3 14.7 %reshape_reshape.3 = bf16[3200,1600]{1,0:T(8,128)(2,1)} reshape(bf16[16,2,100,1600]{3,2,1,0:T(8,128)(2,1)} %copy.104) | data formatting | bytes 20480000 | tf_op jit(solution)/shard_map/reshape;reshape | solution.py:16
  153.0 25.5 %conditional.9 = (f32[64,3200]{1,0:T(8,128)}, f32[64,3200]{1,0:T(8,128)S(1)}, bf16[1,64,3200]{2,1,0:T(8,128)(2,1)S(1)}, bf16[1,64,3200]{2,1,0:T(8,128)(2,1)}, bf...) conditional(s32[]{:T(128)} %convert_element_type.473, () %tuple.151, (bf16[1,64,1600]{2,1,0:T(8,128)(2,1)S(1)}, ...), branch_computations={%region_0.1_spmd, %region_1.5_spmd} | conditional | flops 3289190656 | bytes 78807200 | solution.py:169
  168.0 8.2 %fusion = bf16[64,1600]{0,1:T(8,128)(2,1)S(1)} fusion(bf16[64,3200]{1,0:T(8,128)(2,1)S(1)} %multiply_convert_fusion, bf16[3200,1600]{1,0:T(8,128)(2,1)} %get-tuple-element.500, f32[128,1600]{0,1:T(8,128)S(1)} %fusion.25), kind=kOutput, calls=%fused_computation.1 | convolution fusion | flops 655564800 | bytes 11264000 | tf_op jit(solution)/shard_map/cond/branch_1_fun/dot_general | solution.py:150
  189.0 34.2 %conditional.10 = (bf16[64,1600]{0,1:T(8,128)(2,1)}, bf16[64,1600]{0,1:T(8,128)(2,1)}, f32[1,64,3200]{2,1,0:T(8,128)}, f32[1,64,3200]{2,1,0:T(8,128)}, bf16[1,64...) conditional(s32[]{:T(128)} %convert_element_type.476, ...), branch_computations={%region_5.6_spmd, %region_6.11_spmd} | conditional | flops 3286835456 | bytes 77476808 | solution.py:169
  210.0 9.1 %fusion.36 = bf16[64,1600]{0,1:T(8,128)(2,1)} fusion(bf16[64,3200]{1,0:T(8,128)(2,1)} %get-tuple-element.927, bf16[3200,1600]{1,0:T(8,128)(2,1)} %get-tuple-element.507, bf16[64,1600]{0,1:T(8,128)(2,1)S(1)} %copy-done.21, f32[128,1600]{0,1:T(8,128)S(1)} %fusion.63), kind=kOutput, calls=%fused_computation.50 | convolution fusion | flops 655769600 | bytes 11468800 | tf_op jit(solution)/shard_map/cond/branch_1_fun/dot_general | solution.py:150
  249.0 34.1 %collective-permute-start.5 = (bf16[64,1600]{1,0:T(8,128)(2,1)}, bf16[64,1600]{1,0:T(8,128)(2,1)S(1)}, u32[]{:S(2)}, u32[]{:S(2)}) collective-permute-start(bf16[64,1600]{1,0:T(8,128)(2,1)} %copy.116), channel_id=1, source_target_pairs={{0,32},{32,64},{64,96},{1,33},{33,65},{65,97},{2,34},{34,66},{66,9... | collective-permute-start | bytes 614408 | tf_op jit(solution)/shard_map/ppermute | solution.py:38
  304.8 32.4 %collective-permute-start.6 = (bf16[64,1600]{1,0:T(8,128)(2,1)}, bf16[64,1600]{1,0:T(8,128)(2,1)S(1)}, u32[]{:S(2)}, u32[]{:S(2)}) collective-permute-start(bf16[64,1600]{1,0:T(8,128)(2,1)} %copy.119), channel_id=1, source_target_pairs={{0,32},{32,64},{64,96},{1,33},{33,65},{65,97},{2,34},{34,66},{66,9... | collective-permute-start | bytes 614408 | tf_op jit(solution)/shard_map/ppermute | solution.py:38
  390.1 120.3 %collective-permute-done.13 = bf16[64,1600]{1,0:T(8,128)(2,1)S(1)} collective-permute-done((bf16[64,1600]{1,0:T(8,128)(2,1)S(1)}, bf16[64,1600]{1,0:T(8,128)(2,1)S(1)}, u32[]{:S(2)}, u32[]{:S(2)}) %collective-permute-start.13) | collective-permute-done | bytes 204832 | tf_op jit(solution)/shard_map/ppermute | solution.py:38
  517.7 27.2 %conditional.17 = (bf16[64,1600]{0,1:T(8,128)(2,1)}, bf16[64,1600]{0,1:T(8,128)(2,1)}) conditional(s32[]{:T(128)} %convert_element_type.512, () %tuple.167, (bf16[64,1600]{1,0:T(8,128)(2,1)S(1)}, f32[2,64,3200]{2,1,0:T(8,128)S(1)}, s32[]{:T(128)}, bf16[64,1600]{1,0:T(8,128)(2,1)S(1)}, bf16[3200,1600]{1,0:T(8,128)(2,1)}, ...), branch_computations={%region_59.60_spmd, %region_60.69_spmd} | conditional | flops 3295233024 | bytes 87697088 | solution.py:239
  520.2 7.7 %fusion.369 = f32[128,3200]{1,0:T(8,128)S(1)} fusion(bf16[3200,1600]{1,0:T(8,128)(2,1)} %get-tuple-element.568, bf16[64,1600]{0,1:T(8,128)(2,1)S(1)} %copy.157, bf16[64,1600]{0,1:T(8,128)(2,1)} %copy.156), kind=kOutput, calls=%fused_computation.554 | convolution fusion | flops 1311539200 | bytes 12288000 | tf_op jit(solution)/shard_map/cond/branch_1_fun/dot_general | solution.py:74
  567.0 14.4 %all-to-all-start.2 = ((bf16[32,100,128]{2,1,0:T(8,128)(2,1)}), bf16[32,100,128]{2,1,0:T(8,128)(2,1)}, u32[]{:S(2)}, u32[]{:S(2)}) async-start(bf16[32,100,128]{2,1,0:T(8,128)(2,1)} %all_to_all.36), calls=%async_computation.2 | async-start | bytes 1703936 | tf_op jit(solution)/shard_map/all_to_all | solution.py:250
  583.4 20.7 %all-to-all-done.2 = bf16[32,100,128]{2,1,0:T(8,128)(2,1)} async-done(((bf16[32,100,128]{2,1,0:T(8,128)(2,1)}), bf16[32,100,128]{2,1,0:T(8,128)(2,1)}, u32[]{:S(2)}, u32[]{:S(2)}) %all-to-all-start.2) | async-done | bytes 819232 | tf_op jit(solution)/shard_map/all_to_all | solution.py:250
  614.6 12.2 %all-to-all-done.3 = bf16[32,100,128]{2,1,0:T(8,128)(2,1)S(1)} async-done(((bf16[32,100,128]{2,1,0:T(8,128)(2,1)}), bf16[32,100,128]{2,1,0:T(8,128)(2,1)S(1)}, u32[]{:S(2)}, u32[]{:S(2)}) %all-to-all-start.3) | async-done | bytes 819232 | tf_op jit(solution)/shard_map/all_to_all | solution.py:249
  627.4 51.4 %all-gather.2.cloned.1.call-done = bf16[4096,3200]{1,0:T(8,128)(2,1)} async-done(((bf16[128,3200]{1,0:T(8,128)(2,1)}), bf16[4096,3200]{1,0:T(8,128)(2,1)}) %all-gather.2.cloned.1.call-update) | async-done | bytes 26214416 | tf_op jit(solution)/shard_map/all_gather | solution.py:47
  678.7 9.1 %fusion.378 = f32[100,1600]{1,0:T(8,128)S(1)} fusion(bf16[100,4096]{1,0:T(8,128)(2,1)S(1)} %bitcast.671, bf16[4096,3200]{1,0:T(8,128)(2,1)} %all-gather.2.cloned.1.call-done), kind=kOutput, calls=%fused_computation.573 | convolution fusion | flops 1310720000 | bytes 15090688 | tf_op jit(solution)/shard_map/dot_general | solution.py:254
  695.9 12.1 %fusion.393 = f32[5,5]{1,0:T(8,128)S(1)} fusion(f32[1,1,100,1600]{3,0,2,1:T(1,128)S(1)} %copy.165, f32[1,1,100,1600]{3,0,2,1:T(1,128)S(1)} %bitcast.667, f32[1,1,100,1600]{3,0,2,1:T(1,128)S(1)} %bitcast.673, f32[2,1,100,1600]{3,0,2,1:T(2,128)S(1)} %copy-done.59), kind=kOutput, calls=%fused_computation.589 | convolution fusion | flops 50400000 | bytes 3200100 | tf_op jit(solution)/shard_map/dot_general | solution.py:259
  708.0 9.0 %psum.28 = f32[5,5]{1,0:T(8,128)S(1)} all-reduce(f32[5,5]{1,0:T(8,128)S(1)} %fusion.393), channel_id=1, replica_groups=mesh['section'=4,'dp_0'=4,'dp_1'=4,'dp_2'=2] {'section'}, use_global_device_ids=true, to_apply=%region_69.70 | all-reduce | flops 25 | bytes 200 | tf_op jit(solution)/shard_map/psum | solution.py:51
  717.0 8.4 %psum.29 = f32[5,5]{1,0:T(8,128)S(1)} all-reduce(f32[5,5]{1,0:T(8,128)S(1)} %psum.28), channel_id=1, replica_groups=mesh['section'=4,'dp_0'=4,'dp_1'=4,'dp_2'=2] {'dp_0'}, use_global_device_ids=true, to_apply=%region_70.71 | all-reduce | flops 25 | bytes 200 | tf_op jit(solution)/shard_map/psum | solution.py:51
  731.9 8.4 %psum.31 = f32[5,5]{1,0:T(8,128)S(1)} all-reduce(f32[5,5]{1,0:T(8,128)S(1)} %psum.30), channel_id=1, replica_groups=mesh['section'=4,'dp_0'=4,'dp_1'=4,'dp_2'=2] {'dp_2'}, use_global_device_ids=true, to_apply=%region_72.73 | all-reduce | flops 25 | bytes 200 | tf_op jit(solution)/shard_map/psum | solution.py:51
  (328 shorter events, 272.8 us)
Async XLA Ops:
  11.6 94.1 %all-to-all-start = ((bf16[16,1,100,1600]{3,2,1,0:T(8,128)(2,1)}), bf16[16,1,100,1600]{3,2,1,0:T(8,128)(2,1)}, u32[]{:S(2)}, u32[]{:S(2)}) async-start(bf16[16,1,100,1600]{3,2,1,0:T(8,128)(2,1)} %stack.15), calls=%async_computation | async-start | bytes 11075584 | tf_op jit(solution)/shard_map/all_to_all | solution.py:23
  20.2 658.5 %all-gather.2.cloned.1.call-start = ((), (), s32[]{:S(2)}) async-start(), calls=%async_computation.4 | async-start | bytes 27033600 | tf_op jit(solution)/shard_map/all_gather | solution.py:47
  20.6 17.3 %copy-start.32 = (bf16[128,1600]{1,0:T(8,128)(2,1)}, bf16[128,1600]{1,0:T(8,128)(2,1)S(1)}, u32[]{:S(2)}) copy-start(bf16[128,1600]{1,0:T(8,128)(2,1)S(1)} %copy.101) | copy-start | bytes 1228804
  178.6 5.8 collective-permute-start
  180.0 8.9 %collective-permute-start.1 = (bf16[64,1600]{1,0:T(8,128)(2,1)S(1)}, bf16[64,1600]{1,0:T(8,128)(2,1)S(1)}, u32[]{:S(2)}, u32[]{:S(2)}) collective-permute-start(bf16[64,1600]{1,0:T(8,128)(2,1)S(1)} %get-tuple-element.836), channel_id=1, source_target_pairs={{0,32},{32,64},{64,96},{1,33},{33,65},{65,97},{2,34},{34,66},{66,9... | collective-permute-start | bytes 614408 | tf_op jit(solution)/shard_map/ppermute | solution.py:38
  226.3 10.1 %collective-permute-start.3 = (bf16[64,1600]{1,0:T(8,128)(2,1)}, bf16[64,1600]{1,0:T(8,128)(2,1)S(1)}, u32[]{:S(2)}, u32[]{:S(2)}) collective-permute-start(bf16[64,1600]{1,0:T(8,128)(2,1)} %copy.112), channel_id=1, source_target_pairs={{0,32},{32,64},{64,96},{1,33},{33,65},{65,97},{2,34},{34,66},{66,9... | collective-permute-start | bytes 614408 | tf_op jit(solution)/shard_map/ppermute | solution.py:38
  230.5 8.4 %collective-permute-start.2 = (bf16[64,1600]{1,0:T(8,128)(2,1)S(1)}, bf16[64,1600]{1,0:T(8,128)(2,1)S(1)}, u32[]{:S(2)}, u32[]{:S(2)}) collective-permute-start(bf16[64,1600]{1,0:T(8,128)(2,1)S(1)} %copy.111), channel_id=1, source_target_pairs={{0,32},{32,64},{64,96},{1,33},{33,65},{65,97},{2,34},{34,66},{66,9... | collective-permute-start | bytes 614408 | tf_op jit(solution)/shard_map/ppermute | solution.py:38
  249.0 38.9 %collective-permute-start.5 = (bf16[64,1600]{1,0:T(8,128)(2,1)}, bf16[64,1600]{1,0:T(8,128)(2,1)S(1)}, u32[]{:S(2)}, u32[]{:S(2)}) collective-permute-start(bf16[64,1600]{1,0:T(8,128)(2,1)} %copy.116), channel_id=1, source_target_pairs={{0,32},{32,64},{64,96},{1,33},{33,65},{65,97},{2,34},{34,66},{66,9... | collective-permute-start | bytes 614408 | tf_op jit(solution)/shard_map/ppermute | solution.py:38
  283.2 7.7 %collective-permute-start.4 = (bf16[64,1600]{1,0:T(8,128)(2,1)}, bf16[64,1600]{1,0:T(8,128)(2,1)S(1)}, u32[]{:S(2)}, u32[]{:S(2)}) collective-permute-start(bf16[64,1600]{1,0:T(8,128)(2,1)} %copy.115), channel_id=1, source_target_pairs={{0,32},{32,64},{64,96},{1,33},{33,65},{65,97},{2,34},{34,66},{66,9... | collective-permute-start | bytes 614408 | tf_op jit(solution)/shard_map/ppermute | solution.py:38
  300.8 39.0 %collective-permute-start.7 = (bf16[64,1600]{1,0:T(8,128)(2,1)}, bf16[64,1600]{1,0:T(8,128)(2,1)S(1)}, u32[]{:S(2)}, u32[]{:S(2)}) collective-permute-start(bf16[64,1600]{1,0:T(8,128)(2,1)} %copy.120), channel_id=1, source_target_pairs={{0,32},{32,64},{64,96},{1,33},{33,65},{65,97},{2,34},{34,66},{66,9... | collective-permute-start | bytes 614408 | tf_op jit(solution)/shard_map/ppermute | solution.py:38
  304.8 35.8 %collective-permute-start.6 = (bf16[64,1600]{1,0:T(8,128)(2,1)}, bf16[64,1600]{1,0:T(8,128)(2,1)S(1)}, u32[]{:S(2)}, u32[]{:S(2)}) collective-permute-start(bf16[64,1600]{1,0:T(8,128)(2,1)} %copy.119), channel_id=1, source_target_pairs={{0,32},{32,64},{64,96},{1,33},{33,65},{65,97},{2,34},{34,66},{66,9... | collective-permute-start | bytes 614408 | tf_op jit(solution)/shard_map/ppermute | solution.py:38
  353.6 7.0 collective-permute-start.9
  354.9 9.1 %collective-permute-start.8 = (bf16[64,1600]{1,0:T(8,128)(2,1)S(1)}, bf16[64,1600]{1,0:T(8,128)(2,1)S(1)}, u32[]{:S(2)}, u32[]{:S(2)}) collective-permute-start(bf16[64,1600]{1,0:T(8,128)(2,1)S(1)} %copy.142), channel_id=1, source_target_pairs={{32,0},{64,32},{96,64},{33,1},{65,33},{97,65},{34,2},{66,34},{98,6... | collective-permute-start | bytes 614408 | tf_op jit(solution)/shard_map/ppermute | solution.py:38
  368.8 7.5 collective-permute-start.11
  371.3 9.9 %collective-permute-start.10 = (bf16[64,1600]{1,0:T(8,128)(2,1)S(1)}, bf16[64,1600]{1,0:T(8,128)(2,1)S(1)}, u32[]{:S(2)}, u32[]{:S(2)}) collective-permute-start(bf16[64,1600]{1,0:T(8,128)(2,1)S(1)} %copy.148), channel_id=1, source_target_pairs={{32,0},{64,32},{96,64},{33,1},{65,33},{97,65},{34,2},{66,34},{98,6... | collective-permute-start | bytes 614408 | tf_op jit(solution)/shard_map/ppermute | solution.py:38
  386.1 124.3 %collective-permute-start.13 = (bf16[64,1600]{1,0:T(8,128)(2,1)S(1)}, bf16[64,1600]{1,0:T(8,128)(2,1)S(1)}, u32[]{:S(2)}, u32[]{:S(2)}) collective-permute-start(bf16[64,1600]{1,0:T(8,128)(2,1)S(1)} %copy.155), channel_id=1, source_target_pairs={{32,0},{64,32},{96,64},{33,1},{65,33},{97,65},{34,2},{66,34},{98,6... | collective-permute-start | bytes 614408 | tf_op jit(solution)/shard_map/ppermute | solution.py:38
  388.6 127.2 %collective-permute-start.12 = (bf16[64,1600]{1,0:T(8,128)(2,1)S(1)}, bf16[64,1600]{1,0:T(8,128)(2,1)S(1)}, u32[]{:S(2)}, u32[]{:S(2)}) collective-permute-start(bf16[64,1600]{1,0:T(8,128)(2,1)S(1)} %copy.154), channel_id=1, source_target_pairs={{32,0},{64,32},{96,64},{33,1},{65,33},{97,65},{34,2},{66,34},{98,6... | collective-permute-start | bytes 614408 | tf_op jit(solution)/shard_map/ppermute | solution.py:38
  517.7 35.0 %copy-start.1 = (bf16[2,64,1600]{2,1,0:T(8,128)(2,1)S(1)}, bf16[2,64,1600]{2,1,0:T(8,128)(2,1)}, u32[]{:S(2)}) copy-start(bf16[2,64,1600]{2,1,0:T(8,128)(2,1)} %copy-done) | copy-start | bytes 1228804
  520.2 15.7 %slice-start.10 = ((s8[10240000]{0:T(1024)(128)(4,1)}), s8[4194304]{0:T(1024)(128)(4,1)S(1)}, s32[]{:S(2)}) async-start(s8[10240000]{0:T(1024)(128)(4,1)} %bitcast.624), calls=%async_computation.15 | async-start | bytes 8388608 | tf_op jit(solution)/shard_map/cond
  546.1 6.6 collective-permute-start.15
  548.6 9.8 %collective-permute-start.14 = (bf16[64,1600]{1,0:T(8,128)(2,1)S(1)}, bf16[64,1600]{1,0:T(8,128)(2,1)S(1)}, u32[]{:S(2)}, u32[]{:S(2)}) collective-permute-start(bf16[64,1600]{1,0:T(8,128)(2,1)S(1)} %copy.160), channel_id=1, source_target_pairs={{32,0},{64,32},{96,64},{33,1},{65,33},{97,65},{34,2},{66,34},{98,6... | collective-permute-start | bytes 614408 | tf_op jit(solution)/shard_map/ppermute | solution.py:38
  567.0 37.1 %all-to-all-start.2 = ((bf16[32,100,128]{2,1,0:T(8,128)(2,1)}), bf16[32,100,128]{2,1,0:T(8,128)(2,1)}, u32[]{:S(2)}, u32[]{:S(2)}) async-start(bf16[32,100,128]{2,1,0:T(8,128)(2,1)} %all_to_all.36), calls=%async_computation.2 | async-start | bytes 1703936 | tf_op jit(solution)/shard_map/all_to_all | solution.py:250
  581.5 28.7 %copy-start.30 = (f32[2,1,100,1600]{3,1,2,0:T(1,128)S(1)}, f32[2,1,100,1600]{3,1,2,0:T(1,128)}, u32[]{:S(2)}) copy-start(f32[2,1,100,1600]{3,1,2,0:T(1,128)} %param.36) | copy-start | bytes 3840004
  604.0 22.8 %all-to-all-start.3 = ((bf16[32,100,128]{2,1,0:T(8,128)(2,1)}), bf16[32,100,128]{2,1,0:T(8,128)(2,1)S(1)}, u32[]{:S(2)}, u32[]{:S(2)}) async-start(bf16[32,100,128]{2,1,0:T(8,128)(2,1)} %all_to_all.40), calls=%async_computation.3 | async-start | bytes 1703936 | tf_op jit(solution)/shard_map/all_to_all | solution.py:249
  (44 other events, 279.3 us)
Sparse Core Ops, SparseCore 0:
  562.8 115.8 all-gather.1
